TPU v7x, 32 devices: a whole 2x2x4 slice. The times are simulated.
32 devices in a mesh: expert: 4 (over y, core), shard: 8 (over z, x).
Axes of the slice: x: 2, y: 2, z: 4, core: 2. Of those that a mesh axis runs over, the one named last changes fastest.
Arguments:
- master_gate: float32 [128, 2048, 768], P('expert', 'shard'), may hold values from -0.125 to 0.125
- second_gate: bfloat16 [128, 2048, 768], P('expert', 'shard'), may hold values from -0.0625 to 0.0625
- master_up: float32 [128, 2048, 768], P('expert', 'shard'), may hold values from -0.125 to 0.125
- second_up: bfloat16 [128, 2048, 768], P('expert', 'shard'), may hold values from -0.0625 to 0.0625
- router_weight: float32 [2048, 128], P('shard', 'expert'), may hold values from -0.125 to 0.125
- router_gain: float32 [2048], P('shard'), may hold values from 0.25 to 1.75
Outputs:
- final_gate: bfloat16 [128, 768, 2048], P('expert', 'shard')
- final_up: bfloat16 [128, 768, 2048], P('expert', 'shard')
- serve_router: bfloat16 [2048, 128], replicated
All inputs are finite; a program needn't handle non-finite values.
Results may differ from a plain program's by a relative error of at most 0.001.
Values may be sent and summed in bfloat16 or wider, within the bound.
A program may use at most 192 MiB of HBM per device.

v0:
```python
import jax
import jax.numpy as jnp
from jax import lax
from jax.sharding import PartitionSpec as P


def per_device(master_gate, second_gate, master_up, second_up, router_weight, router_gain):
    merged_gate = master_gate + second_gate.astype(jnp.float32)
    merged_up = master_up + second_up.astype(jnp.float32)
    narrow_gate, narrow_up = (merged_gate.astype(jnp.bfloat16), merged_up.astype(jnp.bfloat16))
    final_gate, final_up = (
        lax.all_to_all(narrow_gate, "shard", split_axis=2, concat_axis=1, tiled=True),
        lax.all_to_all(narrow_up, "shard", split_axis=2, concat_axis=1, tiled=True),
    )
    final_gate = jnp.transpose(final_gate, (0, 2, 1))
    final_up = jnp.transpose(final_up, (0, 2, 1))
    part_router = (router_weight * router_gain[:, None]).astype(jnp.bfloat16)
    row_router = lax.all_gather(part_router, "shard", axis=0, tiled=True)
    serve_router = lax.all_gather(row_router, "expert", axis=1, tiled=True)
    return (final_gate, final_up, serve_router)


def solution(mesh):
    placed = (
        P("expert", "shard", None),
        P("expert", "shard", None),
        P("expert", "shard", None),
        P("expert", "shard", None),
        P("shard", "expert"),
        P("shard"),
    )
    return jax.shard_map(
        per_device,
        mesh=mesh,
        in_specs=placed,
        out_specs=(P("expert", "shard", None), P("expert", "shard", None), P()),
        check_vma=False,
    )
```

profile of v0, /device:TPU:0, one launch (start us, length us, event | category | flops | bytes accessed | tf_op | source)
XLA Modules:
  0.0 713.1 jit_solution(3689968632232905963)
XLA Ops:
  0.6 25.0 %copy.25 = f32[32,256,768]{1,0,2:T(8,128)} copy(f32[32,256,768]{2,1,0:T(8,128)} %param.6) | data formatting | bytes 50331648 | tf_op args[0]
  25.7 16.9 %copy.24 = bf16[32,256,768]{1,0,2:T(8,128)(2,1)} copy(bf16[32,256,768]{2,1,0:T(8,128)(2,1)} %param.7) | data formatting | bytes 25165824 | tf_op args[1]
  42.5 17.3 %add_convert_fusion.1 = bf16[32,256,768]{1,0,2:T(8,128)(2,1)} fusion(f32[32,256,768]{1,0,2:T(8,128)} %copy.25, bf16[32,256,768]{1,0,2:T(8,128)(2,1)} %copy.24), kind=kLoop, calls=%fused_computation.1 | loop fusion | flops 18874368 | bytes 50331648 | tf_op jit(solution)/shard_map/convert_element_type | solution.py:10
  59.8 7.3 %all-to-all-start = ((bf16[32,256,768]{1,0,2:T(8,128)(2,1)}), bf16[32,256,768]{1,0,2:T(8,128)(2,1)}, u32[]{:S(2)}, u32[]{:S(2)}) async-start(bf16[32,256,768]{1,0,2:T(8,128)(2,1)} %add_convert_fusion.1), calls=%async_computation | async-start | bytes 25165824 | tf_op jit(solution)/shard_map/all_to_all | solution.py:12
  67.1 25.0 %copy.29 = f32[32,256,768]{1,0,2:T(8,128)} copy(f32[32,256,768]{2,1,0:T(8,128)} %param.8) | data formatting | bytes 50331648 | tf_op args[2]
  92.2 16.9 %copy.28 = bf16[32,256,768]{1,0,2:T(8,128)(2,1)} copy(bf16[32,256,768]{2,1,0:T(8,128)(2,1)} %param.9) | data formatting | bytes 25165824 | tf_op args[3]
  109.0 17.3 %add_convert_fusion = bf16[32,256,768]{1,0,2:T(8,128)(2,1)} fusion(f32[32,256,768]{1,0,2:T(8,128)} %copy.29, bf16[32,256,768]{1,0,2:T(8,128)(2,1)} %copy.28), kind=kLoop, calls=%fused_computation | loop fusion | flops 18874368 | bytes 50331648 | tf_op jit(solution)/shard_map/convert_element_type | solution.py:10
  126.3 0.0 copy-start
  126.3 0.0 copy-start.1
  126.3 213.9 %all-to-all-done = bf16[32,256,768]{1,0,2:T(8,128)(2,1)} async-done(((bf16[32,256,768]{1,0,2:T(8,128)(2,1)}), bf16[32,256,768]{1,0,2:T(8,128)(2,1)}, u32[]{:S(2)}, u32[]{:S(2)}) %all-to-all-start) | async-done | bytes 12582944 | tf_op jit(solution)/shard_map/all_to_all | solution.py:12
  340.2 5.3 all-to-all-start.1
  345.5 0.0 copy-done
  345.5 0.0 copy-done.1
  345.6 292.2 %all_gather.6 = bf16[2048,32]{0,1:T(8,128)(2,1)S(1)} all-gather(bf16[256,32]{0,1:T(8,128)(2,1)S(1)} %multiply_convert_fusion), channel_id=1, replica_groups=mesh['expert'=4,'shard'=8] {'shard'}, dimensions={0}, use_global_device_ids=true | all-gather | bytes 147456 | tf_op jit(solution)/shard_map/all_gather | solution.py:18
  637.8 7.2 %all_gather.7 = bf16[2048,128]{0,1:T(8,128)(2,1)S(1)} all-gather(bf16[2048,32]{0,1:T(8,128)(2,1)S(1)} %all_gather.6), channel_id=1, replica_groups=mesh['expert'=4,'shard'=8] {'expert'}, dimensions={1}, use_global_device_ids=true | all-gather | bytes 655360 | tf_op jit(solution)/shard_map/all_gather | solution.py:19
  645.0 1.0 copy.32
  646.0 14.1 %copy.27 = bf16[32,8,256,96]{2,1,3,0:T(8,128)(2,1)} copy(bf16[32,8,256,96]{2,0,3,1:T(8,128)(2,1)} %bitcast.2) | data formatting | bytes 25165824 | tf_op jit(solution)/shard_map/all_to_all | solution.py:12
  660.0 19.5 %all_to_all.29 = bf16[32,2048,96]{1,2,0:T(8,128)(2,1)} reshape(bf16[32,8,256,96]{2,1,3,0:T(8,128)(2,1)} %copy.27) | data formatting | bytes 25165824 | tf_op jit(solution)/shard_map/all_to_all | solution.py:12
  679.5 0.0 all-to-all-done.1
  679.5 14.1 %copy.31 = bf16[32,8,256,96]{2,1,3,0:T(8,128)(2,1)} copy(bf16[32,8,256,96]{2,0,3,1:T(8,128)(2,1)} %bitcast.6) | data formatting | bytes 25165824 | tf_op jit(solution)/shard_map/all_to_all | solution.py:13
  693.6 19.5 %all_to_all.33 = bf16[32,2048,96]{1,2,0:T(8,128)(2,1)} reshape(bf16[32,8,256,96]{2,1,3,0:T(8,128)(2,1)} %copy.31) | data formatting | bytes 25165824 | tf_op jit(solution)/shard_map/all_to_all | solution.py:13
  (1 shorter events, 0.0 us)
Async XLA Ops:
  59.8 280.3 %all-to-all-start = ((bf16[32,256,768]{1,0,2:T(8,128)(2,1)}), bf16[32,256,768]{1,0,2:T(8,128)(2,1)}, u32[]{:S(2)}, u32[]{:S(2)}) async-start(bf16[32,256,768]{1,0,2:T(8,128)(2,1)} %add_convert_fusion.1), calls=%async_computation | async-start | bytes 25165824 | tf_op jit(solution)/shard_map/all_to_all | solution.py:12
  126.3 219.2 %copy-start = (f32[256,32]{0,1:T(8,128)S(1)}, f32[256,32]{0,1:T(8,128)}, u32[]{:S(2)}) copy-start(f32[256,32]{0,1:T(8,128)} %param.10) | copy-start | bytes 98308
  126.3 219.2 %copy-start.1 = (f32[256]{0:T(256)S(1)}, f32[256]{0:T(256)}, u32[]{:S(2)}) copy-start(f32[256]{0:T(256)} %param.11) | copy-start | bytes 3076
  340.2 339.3 %all-to-all-start.1 = ((bf16[32,256,768]{1,0,2:T(8,128)(2,1)}), bf16[32,256,768]{1,0,2:T(8,128)(2,1)}, u32[]{:S(2)}, u32[]{:S(2)}) async-start(bf16[32,256,768]{1,0,2:T(8,128)(2,1)} %add_convert_fusion), calls=%async_computation.1 | async-start | bytes 25165824 | tf_op jit(solution)/shard_map/all_to_all | solution.py:13
where the time goes:
time: 716 us; the launch traced here: 713 us
  blocking collectives  299 us (42%)
  waiting for transfers between devices  214 us (30%)
  local copies, waits for them, and re-layouts  152 us (21%)
  other arithmetic  34.6 us (5%)
  starting transfers between devices  12.6 us (2%)
    all_gather x1, blocking collectives, per_device(): row_router = lax.all_gather(part_router, 'shard', axis=0, tiled=True)  292 us
    all_to_all x1, waiting for transfers between devices, per_device(): lax.all_to_all(narrow_gate, 'shard', split_axis=2, concat_axis=1, tiled=T...  214 us
    unnamed x9, local copies, waits for them, and re-layouts  84.8 us
    all_to_all x2, local copies, waits for them, and re-layouts, per_device(): lax.all_to_all(narrow_up, 'shard', split_axis=2, concat_axis=1, tiled=True)  33.6 us
    all_to_all x2, local copies, waits for them, and re-layouts, per_device(): lax.all_to_all(narrow_gate, 'shard', split_axis=2, concat_axis=1, tiled=T...  33.5 us
    convert_element_type x1, other arithmetic, per_device(): merged_gate.astype(jnp.bfloat16)  17.3 us
    convert_element_type x1, other arithmetic, per_device(): merged_up.astype(jnp.bfloat16)  17.3 us
  transfers between devices with their start and end apart: 2, of which 1 were waited for; matrix products, arithmetic and copies ran while one was open for 10% of the time, Pallas kernels for 0%

commit v1 on v0

--- a/solution.py
+++ b/solution.py
@@ -16,7 +16,7 @@
     final_up = jnp.transpose(final_up, (0, 2, 1))
     part_router = (router_weight * router_gain[:, None]).astype(jnp.bfloat16)
     row_router = lax.all_gather(part_router, "shard", axis=0, tiled=True)
-    serve_router = lax.all_gather(row_router, "expert", axis=1, tiled=True)
+    serve_router = jnp.concatenate(lax.all_gather(row_router, "expert"), axis=1)
     return (final_gate, final_up, serve_router)
 
 

time: 716 us -> 717 us (level)
  no operation moved by 1% of the time
where the time goes in v1:
time: 717 us; the launch traced here: 714 us
  blocking collectives  299 us (42%)
  waiting for transfers between devices  214 us (30%)
  local copies, waits for them, and re-layouts  153 us (21%)
  other arithmetic  34.6 us (5%)
  starting transfers between devices  12.6 us (2%)
    all_gather x1, blocking collectives, per_device(): row_router = lax.all_gather(part_router, 'shard', axis=0, tiled=True)  292 us
    all_to_all x1, waiting for transfers between devices, per_device(): lax.all_to_all(narrow_gate, 'shard', split_axis=2, concat_axis=1, tiled=T...  214 us
    unnamed x9, local copies, waits for them, and re-layouts  84.8 us
    all_to_all x2, local copies, waits for them, and re-layouts, per_device(): lax.all_to_all(narrow_up, 'shard', split_axis=2, concat_axis=1, tiled=True)  33.6 us
    all_to_all x2, local copies, waits for them, and re-layouts, per_device(): lax.all_to_all(narrow_gate, 'shard', split_axis=2, concat_axis=1, tiled=T...  33.5 us
    convert_element_type x1, other arithmetic, per_device(): merged_gate.astype(jnp.bfloat16)  17.3 us
    convert_element_type x1, other arithmetic, per_device(): merged_up.astype(jnp.bfloat16)  17.3 us
  transfers between devices with their start and end apart: 2, of which 1 were waited for; matrix products, arithmetic and copies ran while one was open for 10% of the time, Pallas kernels for 0%

profile of v1, /device:TPU:0, one launch (start us, length us, event | category | flops | bytes accessed | tf_op | source)
XLA Modules:
  0.0 713.7 jit_solution(1268818955185201082)
XLA Ops:
  0.6 25.0 %copy.26 = f32[32,256,768]{1,0,2:T(8,128)} copy(f32[32,256,768]{2,1,0:T(8,128)} %param.6) | data formatting | bytes 50331648 | tf_op args[0]
  25.7 16.9 %copy.25 = bf16[32,256,768]{1,0,2:T(8,128)(2,1)} copy(bf16[32,256,768]{2,1,0:T(8,128)(2,1)} %param.7) | data formatting | bytes 25165824 | tf_op args[1]
  42.5 17.3 %add_convert_fusion.1 = bf16[32,256,768]{1,0,2:T(8,128)(2,1)} fusion(f32[32,256,768]{1,0,2:T(8,128)} %copy.26, bf16[32,256,768]{1,0,2:T(8,128)(2,1)} %copy.25), kind=kLoop, calls=%fused_computation.1 | loop fusion | flops 18874368 | bytes 50331648 | tf_op jit(solution)/shard_map/convert_element_type | solution.py:10
  59.8 7.3 %all-to-all-start = ((bf16[32,256,768]{1,0,2:T(8,128)(2,1)}), bf16[32,256,768]{1,0,2:T(8,128)(2,1)}, u32[]{:S(2)}, u32[]{:S(2)}) async-start(bf16[32,256,768]{1,0,2:T(8,128)(2,1)} %add_convert_fusion.1), calls=%async_computation | async-start | bytes 25165824 | tf_op jit(solution)/shard_map/all_to_all | solution.py:12
  67.1 25.0 %copy.30 = f32[32,256,768]{1,0,2:T(8,128)} copy(f32[32,256,768]{2,1,0:T(8,128)} %param.8) | data formatting | bytes 50331648 | tf_op args[2]
  92.2 16.9 %copy.29 = bf16[32,256,768]{1,0,2:T(8,128)(2,1)} copy(bf16[32,256,768]{2,1,0:T(8,128)(2,1)} %param.9) | data formatting | bytes 25165824 | tf_op args[3]
  109.0 17.3 %add_convert_fusion = bf16[32,256,768]{1,0,2:T(8,128)(2,1)} fusion(f32[32,256,768]{1,0,2:T(8,128)} %copy.30, bf16[32,256,768]{1,0,2:T(8,128)(2,1)} %copy.29), kind=kLoop, calls=%fused_computation | loop fusion | flops 18874368 | bytes 50331648 | tf_op jit(solution)/shard_map/convert_element_type | solution.py:10
  126.3 0.0 copy-start
  126.3 0.0 copy-start.1
  126.3 213.9 %all-to-all-done = bf16[32,256,768]{1,0,2:T(8,128)(2,1)} async-done(((bf16[32,256,768]{1,0,2:T(8,128)(2,1)}), bf16[32,256,768]{1,0,2:T(8,128)(2,1)}, u32[]{:S(2)}, u32[]{:S(2)}) %all-to-all-start) | async-done | bytes 12582944 | tf_op jit(solution)/shard_map/all_to_all | solution.py:12
  340.2 5.3 all-to-all-start.1
  345.5 0.0 copy-done
  345.5 0.0 copy-done.1
  345.6 292.2 %all_gather.9 = bf16[2048,32]{0,1:T(8,128)(2,1)S(1)} all-gather(bf16[256,32]{0,1:T(8,128)(2,1)S(1)} %multiply_convert_fusion), channel_id=1, replica_groups=mesh['expert'=4,'shard'=8] {'shard'}, dimensions={0}, use_global_device_ids=true | all-gather | bytes 147456 | tf_op jit(solution)/shard_map/all_gather | solution.py:18
  637.8 7.2 %all-gather = bf16[8192,32]{0,1:T(8,128)(2,1)S(1)} all-gather(bf16[2048,32]{0,1:T(8,128)(2,1)S(1)} %all_gather.9), channel_id=2, replica_groups=mesh['expert'=4,'shard'=8] {'expert'}, dimensions={0}, use_global_device_ids=true | all-gather | bytes 655360 | tf_op jit(solution)/shard_map/all_gather | solution.py:19
  645.0 0.4 reshape.15
  645.3 0.3 copy.33
  645.6 1.0 copy.34
  646.6 14.1 %copy.28 = bf16[32,8,256,96]{2,1,3,0:T(8,128)(2,1)} copy(bf16[32,8,256,96]{2,0,3,1:T(8,128)(2,1)} %bitcast.2) | data formatting | bytes 25165824 | tf_op jit(solution)/shard_map/all_to_all | solution.py:12
  660.7 19.5 %all_to_all.29 = bf16[32,2048,96]{1,2,0:T(8,128)(2,1)} reshape(bf16[32,8,256,96]{2,1,3,0:T(8,128)(2,1)} %copy.28) | data formatting | bytes 25165824 | tf_op jit(solution)/shard_map/all_to_all | solution.py:12
  680.2 0.0 all-to-all-done.1
  680.2 14.1 %copy.32 = bf16[32,8,256,96]{2,1,3,0:T(8,128)(2,1)} copy(bf16[32,8,256,96]{2,0,3,1:T(8,128)(2,1)} %bitcast.6) | data formatting | bytes 25165824 | tf_op jit(solution)/shard_map/all_to_all | solution.py:13
  694.3 19.5 %all_to_all.33 = bf16[32,2048,96]{1,2,0:T(8,128)(2,1)} reshape(bf16[32,8,256,96]{2,1,3,0:T(8,128)(2,1)} %copy.32) | data formatting | bytes 25165824 | tf_op jit(solution)/shard_map/all_to_all | solution.py:13
  (1 shorter events, 0.0 us)
Async XLA Ops:
  59.8 280.3 %all-to-all-start = ((bf16[32,256,768]{1,0,2:T(8,128)(2,1)}), bf16[32,256,768]{1,0,2:T(8,128)(2,1)}, u32[]{:S(2)}, u32[]{:S(2)}) async-start(bf16[32,256,768]{1,0,2:T(8,128)(2,1)} %add_convert_fusion.1), calls=%async_computation | async-start | bytes 25165824 | tf_op jit(solution)/shard_map/all_to_all | solution.py:12
  126.3 219.2 %copy-start = (f32[256,32]{0,1:T(8,128)S(1)}, f32[256,32]{0,1:T(8,128)}, u32[]{:S(2)}) copy-start(f32[256,32]{0,1:T(8,128)} %param.10) | copy-start | bytes 98308
  126.3 219.2 %copy-start.1 = (f32[256]{0:T(256)S(1)}, f32[256]{0:T(256)}, u32[]{:S(2)}) copy-start(f32[256]{0:T(256)} %param.11) | copy-start | bytes 3076
  340.2 340.0 %all-to-all-start.1 = ((bf16[32,256,768]{1,0,2:T(8,128)(2,1)}), bf16[32,256,768]{1,0,2:T(8,128)(2,1)}, u32[]{:S(2)}, u32[]{:S(2)}) async-start(bf16[32,256,768]{1,0,2:T(8,128)(2,1)} %add_convert_fusion), calls=%async_computation.1 | async-start | bytes 25165824 | tf_op jit(solution)/shard_map/all_to_all | solution.py:13
